TPU v7x, 32 devices: a whole 2x2x4 slice. The times are simulated.
32 devices in a mesh: section: 4 (over z), shard: 8 (over y, x, core).
Axes of the slice: x: 2, y: 2, z: 4, core: 2. Of those that a mesh axis runs over, the one named last changes fastest.
Arguments:
- grad_parts: bfloat16 [4, 8, 256, 8192], P('section', 'shard'), may hold values from -6 to 6
- params: bfloat16 [4, 256, 8192], P('section', 'shard'), may hold values from -6 to 6
- moment_first: float32 [4, 256, 8192], P('section', 'shard'), may hold values from -6 to 6
- moment_second: float32 [4, 256, 8192], P('section', 'shard'), may hold values from 0.5 to 50
- block_layer: int32 [4, 32], P('section', 'shard'), may hold values from 0 to 7, as said below
- block_valid: int32 [4, 32], P('section', 'shard'), may hold values from 0 to 1
- decay: float32 [8], replicated, may hold values from 0.05 to 1
Outputs:
- new_params: bfloat16 [4, 256, 8192], P('section', 'shard')
- new_first: float32 [4, 256, 8192], P('section', 'shard')
- new_second: float32 [4, 256, 8192], P('section', 'shard')
- ratios: float32 [8], replicated
Inputs may be any that keep to these rules, and one draw needn't show every extreme that they name: `block_layer`: in every section the live slots come first. One section has all 32 slots live; each other section has between 16 and 32 live slots, and all sections together have 3 * 32. Over the live slots taken section by section in order, layer ids never fall and every layer has exactly 12 live slots; dead slots hold arbitrary layer ids.
All inputs are finite; a program needn't handle non-finite values.
Results may differ from a plain program's by a relative error of at most 0.008.
Values may be sent and summed in bfloat16 or wider, within the bound.
No kernel may reach another device: no remote copies, remote signals or barrier semaphores. Data moves between devices by JAX's collectives and lax.ppermute only.
A program may use at most 64 MiB of HBM per device.

v0:
```python
import jax
import jax.numpy as jnp
from jax import lax
from jax.sharding import PartitionSpec as P

bias_first = 1.0 - 0.9**10
bias_second = 1.0 - 0.99**10


def carried_in(part, axis, combine, identity):
    place = lax.axis_index(axis)
    gathered = lax.all_gather(part, axis)
    state = jnp.zeros_like(part) + jnp.asarray(identity, part.dtype)

    def one(step, state):
        return combine(state, lax.dynamic_index_in_dim(gathered, step, 0, False))

    return lax.fori_loop(0, place, one, state)


def from_root(block, axis, source):
    block = jnp.where(lax.axis_index(axis) == source, block, jnp.zeros_like(block))
    return lax.psum(block, axis)


def combine_sum(earlier, later):
    return earlier + later


def shards(grad_parts, params, moment_first, moment_second, block_layer, block_valid, decay):
    row_count = params.shape[1]
    local_grad = grad_parts[0, 0]
    gradient = lax.psum_scatter(
        local_grad.astype(jnp.float32).astype(jnp.bfloat16),
        "shard",
        scatter_dimension=0,
        tiled=True,
    ).astype(jnp.float32)
    block_rows = row_count // block_layer.shape[1]
    layer_rows = jnp.repeat(block_layer[0], block_rows)
    valid_rows = jnp.repeat(block_valid[0], block_rows) > 0
    layer_ids = jnp.arange(decay.shape[0], dtype=jnp.int32)
    onehot = jnp.where(
        valid_rows[:, None] & (layer_rows[:, None] == layer_ids[None, :]), 1.0, 0.0
    ).astype(jnp.float32)
    weights = params[0].astype(jnp.float32)
    first = 0.9 * moment_first[0] + 0.1 * gradient
    second = 0.99 * moment_second[0] + 0.01 * gradient * gradient
    row_decay = jnp.dot(onehot, decay, precision=lax.Precision.HIGHEST)
    update = (
        first / bias_first / (jnp.sqrt(second / bias_second) + 1e-06) + row_decay[:, None] * weights
    )
    row_sums = jnp.stack(
        [jnp.sum(weights * weights, axis=-1), jnp.sum(update * update, axis=-1)], axis=1
    )
    partial_value = jnp.dot(onehot.T, row_sums, precision=lax.Precision.HIGHEST)
    section_total = lax.psum(partial_value, "shard")
    before = carried_in(section_total, "section", combine_sum, jnp.zeros_like(section_total))
    through = before + section_total
    totals = from_root(through, "section", lax.axis_size("section") - 1)
    ratios = jnp.sqrt(totals[:, 0] / (totals[:, 1] + 1.0))
    row_ratio = jnp.dot(onehot, ratios, precision=lax.Precision.HIGHEST)
    stepped = weights - 0.1 * row_ratio[:, None] * update
    live = valid_rows[:, None]
    new_params = jnp.where(live, stepped, weights).astype(jnp.bfloat16)
    new_first = jnp.where(live, first, moment_first[0])
    new_second = jnp.where(live, second, moment_second[0])
    return (new_params[None], new_first[None], new_second[None], ratios)


def solution(mesh):
    placed = (
        P("section", "shard", None, None),
        P("section", "shard", None),
        P("section", "shard", None),
        P("section", "shard", None),
        P("section", "shard"),
        P("section", "shard"),
        P(),
    )
    return jax.shard_map(
        shards,
        mesh=mesh,
        in_specs=placed,
        out_specs=(
            P("section", "shard", None),
            P("section", "shard", None),
            P("section", "shard", None),
            P(),
        ),
        check_vma=False,
    )
```

profile of v0, /device:TPU:0, one launch (start us, length us, event | category | flops | bytes accessed | tf_op | source)
XLA Modules:
  0.0 109.7 jit_solution(5550758126043738490)
XLA Ops:
  7.2 0.0 copy-start
  7.2 0.0 copy-start.4
  7.2 0.0 copy-start.3
  7.2 0.0 copy-start.1
  7.2 0.0 copy-start.2
  7.2 0.0 reduce-scatter.2.cloned.1.call-start
  7.3 0.7 reduce-scatter.2.cloned.1.call-update
  8.0 0.0 copy-done.4
  8.0 0.1 broadcast_in_dim.42
  8.1 0.1 gt.20
  8.1 0.0 copy-done.3
  8.1 0.1 broadcast_in_dim.44
  8.2 0.1 eq.18
  8.3 0.0 copy-done
  8.3 0.2 convolution_bitcast_fusion.1
  8.5 56.8 %reduce-scatter.2.cloned.1.call-done = bf16[32,8192]{1,0:T(8,128)(2,1)} async-done(((bf16[256,8192]{1,0:T(8,128)(2,1)}), bf16[32,8192]{1,0:T(8,128)(2,1)}) %reduce-scatter.2.cloned.1.call-update) | async-done | bytes 524304 | tf_op jit(solution)/shard_map/reduce_scatter | solution.py:33
  65.3 0.0 copy-done.1
  65.3 0.0 copy-done.2
  65.3 3.8 %multiply_reduce_fusion = (f32[32]{0:T(128)S(1)}, f32[32,8192]{1,0:T(8,128)S(1)}, f32[1,32,8192]{2,1,0:T(8,128)}, f32[1,32,8192]{2,1,0:T(8,128)}, f32[32]{0:T(128)S(1)}) fusion(bf16[1,32,8192]{2,1,0:T(8,128)(2,1)S(1)} %copy-done.1, f32[32]{0:T(128)S(1)} %convolution_bitcast_fusion.1, f32[1,32,8192]{2,1,0:T(8,128)S(1)} %copy-done.2, ...), kind=kLoop, calls=%fused_computation.26 | loop fusion | flops 5504960 | bytes 6291872 | tf_op jit(solution)/shard_map/reduce_sum | solution.py:54
  69.1 0.2 fusion.15
  69.3 12.5 %psum.14 = f32[8,2]{0,1:T(2,128)S(1)} all-reduce(f32[8,2]{0,1:T(2,128)S(1)} %fusion.15), channel_id=1, replica_groups=mesh['section'=4,'shard'=8] {'shard'}, use_global_device_ids=true, to_apply=%region_3.4 | all-reduce | flops 16 | bytes 128 | tf_op jit(solution)/shard_map/psum | solution.py:57
  81.8 10.9 %all-gather.1 = f32[4,8,2]{1,2,0:T(2,128)S(1)} all-gather(f32[1,8,2]{1,2,0:T(2,128)S(1)} %bitcast.70), channel_id=2, replica_groups=mesh['section'=4,'shard'=8] {'section'}, dimensions={0}, use_global_device_ids=true | all-gather | bytes 320 | tf_op jit(solution)/shard_map/all_gather | solution.py:12
  92.7 8.4 %psum.15 = f32[8,2]{0,1:T(2,128)S(1)} all-reduce(f32[8,2]{0,1:T(2,128)S(1)} %add_select_fusion), channel_id=1, replica_groups=mesh['section'=4,'shard'=8] {'section'}, use_global_device_ids=true, to_apply=%region_6.7 | all-reduce | flops 16 | bytes 128 | tf_op jit(solution)/shard_map/psum | solution.py:23
  101.1 0.2 fusion
  101.3 0.5 fusion.48
  101.8 1.0 fusion.13
  (4 shorter events, 0.0 us)
Async XLA Ops:
  7.2 1.1 %copy-start = (f32[8]{0:T(128)S(1)}, f32[8]{0:T(128)}, u32[]{:S(2)}) copy-start(f32[8]{0:T(128)} %param.15) | copy-start | bytes 100
  7.2 0.8 copy-start.4
  7.2 1.0 copy-start.3
  7.2 58.1 %copy-start.1 = (bf16[1,32,8192]{2,1,0:T(8,128)(2,1)S(1)}, bf16[1,32,8192]{2,1,0:T(8,128)(2,1)}, u32[]{:S(2)}) copy-start(bf16[1,32,8192]{2,1,0:T(8,128)(2,1)} %param.10) | copy-start | bytes 1572868
  7.2 58.1 %copy-start.2 = (f32[1,32,8192]{2,1,0:T(8,128)S(1)}, f32[1,32,8192]{2,1,0:T(8,128)}, u32[]{:S(2)}) copy-start(f32[1,32,8192]{2,1,0:T(8,128)} %param.12) | copy-start | bytes 3145732
  7.2 58.1 %reduce-scatter.2.cloned.1.call-start = ((), (), s32[]{:S(2)}) async-start(), calls=%async_computation.1 | async-start | bytes 4718592 | tf_op jit(solution)/shard_map/reduce_scatter | solution.py:33
Sparse Core Ops, SparseCore 0:
  11.4 53.8 reduce-scatter.1
where the time goes:
time: 110 us
  waiting for transfers between devices  57.5 us (52%)
  blocking collectives  31.8 us (29%)
  between operations  14.1 us (13%)
  other arithmetic  5.4 us (5%)
    reduce_scatter x1, waiting for transfers between devices, shards(): lax.psum_scatter(local_grad.astype(jnp.float32).astype(jnp.bfloat16), 'sh...  56.8 us
    psum x1, blocking collectives, shards(): section_total = lax.psum(partial_value, 'shard')  12.5 us
    all_gather x1, blocking collectives, carried_in(): gathered = lax.all_gather(part, axis)  10.9 us
    psum x1, blocking collectives, from_root(): return lax.psum(block, axis)  8.37 us
    reduce_sum x1, other arithmetic, shards(): jnp.sum(update * update, axis=-1)  3.8 us
  transfers between devices with their start and end apart: 1, of which 1 were waited for; matrix products, arithmetic and copies ran while one was open for 0% of the time, Pallas kernels for 0%

commit v1 on v0

--- a/solution.py
+++ b/solution.py
@@ -54,7 +54,7 @@
         [jnp.sum(weights * weights, axis=-1), jnp.sum(update * update, axis=-1)], axis=1
     )
     partial_value = jnp.dot(onehot.T, row_sums, precision=lax.Precision.HIGHEST)
-    section_total = lax.psum(partial_value, "shard")
+    section_total = jnp.sum(lax.all_gather(partial_value, "shard"), axis=0)
     before = carried_in(section_total, "section", combine_sum, jnp.zeros_like(section_total))
     through = before + section_total
     totals = from_root(through, "section", lax.axis_size("section") - 1)

time: 110 us -> 106 us (0.964)
  blocking collectives: 31.8 us -> 28.1 us
    psum x1 -> x0, blocking collectives: 12.5 us -> none  [shards(): section_total = lax.psum(partial_value, 'shard')]
    all_gather x0 -> x1, blocking collectives: none -> 8.87 us  [shards(): section_total = jnp.sum(lax.all_gather(partial_value, 'shard'), axis=0)]
where the time goes in v1:
time: 106 us
  waiting for transfers between devices  57.5 us (54%)
  blocking collectives  28.1 us (27%)
  between operations  14.1 us (13%)
  other arithmetic  5.42 us (5%)
    reduce_scatter x1, waiting for transfers between devices, shards(): lax.psum_scatter(local_grad.astype(jnp.float32).astype(jnp.bfloat16), 'sh...  56.8 us
    all_gather x1, blocking collectives, carried_in(): gathered = lax.all_gather(part, axis)  10.9 us
    all_gather x1, blocking collectives, shards(): section_total = jnp.sum(lax.all_gather(partial_value, 'shard'), axis=0)  8.87 us
    psum x1, blocking collectives, from_root(): return lax.psum(block, axis)  8.37 us
    reduce_sum x1, other arithmetic, shards(): jnp.sum(update * update, axis=-1)  3.8 us
  transfers between devices with their start and end apart: 1, of which 1 were waited for; matrix products, arithmetic and copies ran while one was open for 0% of the time, Pallas kernels for 0%

profile of v1, /device:TPU:0, one launch (start us, length us, event | category | flops | bytes accessed | tf_op | source)
XLA Modules:
  0.0 106.1 jit_solution(11892992813210922322)
XLA Ops:
  7.2 0.0 copy-start
  7.2 0.0 copy-start.4
  7.2 0.0 copy-start.3
  7.2 0.0 copy-start.1
  7.2 0.0 copy-start.2
  7.2 0.0 reduce-scatter.2.cloned.1.call-start
  7.3 0.7 reduce-scatter.2.cloned.1.call-update
  8.0 0.0 copy-done.4
  8.0 0.1 broadcast_in_dim.42
  8.1 0.1 gt.20
  8.1 0.0 copy-done.3
  8.2 0.1 broadcast_in_dim.44
  8.2 0.1 eq.18
  8.3 0.0 copy-done
  8.3 0.2 convolution_bitcast_fusion.2
  8.5 56.8 %reduce-scatter.2.cloned.1.call-done = bf16[32,8192]{1,0:T(8,128)(2,1)} async-done(((bf16[256,8192]{1,0:T(8,128)(2,1)}), bf16[32,8192]{1,0:T(8,128)(2,1)}) %reduce-scatter.2.cloned.1.call-update) | async-done | bytes 524304 | tf_op jit(solution)/shard_map/reduce_scatter | solution.py:33
  65.3 0.0 copy-done.1
  65.3 0.0 copy-done.2
  65.3 3.8 %multiply_reduce_fusion = (f32[32]{0:T(128)S(1)}, f32[32,8192]{1,0:T(8,128)S(1)}, f32[1,32,8192]{2,1,0:T(8,128)}, f32[1,32,8192]{2,1,0:T(8,128)}, f32[32]{0:T(128)S(1)}) fusion(bf16[1,32,8192]{2,1,0:T(8,128)(2,1)S(1)} %copy-done.1, f32[32]{0:T(128)S(1)} %convolution_bitcast_fusion.2, f32[1,32,8192]{2,1,0:T(8,128)S(1)} %copy-done.2, ...), kind=kLoop, calls=%fused_computation.27 | loop fusion | flops 5504960 | bytes 6291872 | tf_op jit(solution)/shard_map/reduce_sum | solution.py:54
  69.1 0.2 convolution_bitcast_fusion
  69.3 8.9 %all-gather.2 = f32[8,8,2]{1,2,0:T(2,128)S(1)} all-gather(f32[1,8,2]{1,2,0:T(2,128)S(1)} %convolution_bitcast_fusion), channel_id=2, replica_groups=mesh['section'=4,'shard'=8] {'shard'}, dimensions={0}, use_global_device_ids=true | all-gather | bytes 576 | tf_op jit(solution)/shard_map/all_gather | solution.py:57
  78.2 10.9 %all-gather.3 = f32[4,8,2]{1,2,0:T(2,128)S(1)} all-gather(f32[1,8,2]{1,2,0:T(2,128)S(1)} %bitcast.72), channel_id=3, replica_groups=mesh['section'=4,'shard'=8] {'section'}, dimensions={0}, use_global_device_ids=true | all-gather | bytes 320 | tf_op jit(solution)/shard_map/all_gather | solution.py:12
  89.1 8.4 %psum.7 = f32[8,2]{0,1:T(2,128)S(1)} all-reduce(f32[8,2]{0,1:T(2,128)S(1)} %add_select_fusion), channel_id=1, replica_groups=mesh['section'=4,'shard'=8] {'section'}, use_global_device_ids=true, to_apply=%region_6.7 | all-reduce | flops 16 | bytes 128 | tf_op jit(solution)/shard_map/psum | solution.py:23
  97.5 0.2 fusion
  97.7 0.5 fusion.47
  98.2 1.0 fusion.13
  (5 shorter events, 0.0 us)
Async XLA Ops:
  7.2 1.1 %copy-start = (f32[8]{0:T(128)S(1)}, f32[8]{0:T(128)}, u32[]{:S(2)}) copy-start(f32[8]{0:T(128)} %param.15) | copy-start | bytes 100
  7.2 0.8 copy-start.4
  7.2 1.0 copy-start.3
  7.2 58.1 %copy-start.1 = (bf16[1,32,8192]{2,1,0:T(8,128)(2,1)S(1)}, bf16[1,32,8192]{2,1,0:T(8,128)(2,1)}, u32[]{:S(2)}) copy-start(bf16[1,32,8192]{2,1,0:T(8,128)(2,1)} %param.10) | copy-start | bytes 1572868
  7.2 58.1 %copy-start.2 = (f32[1,32,8192]{2,1,0:T(8,128)S(1)}, f32[1,32,8192]{2,1,0:T(8,128)}, u32[]{:S(2)}) copy-start(f32[1,32,8192]{2,1,0:T(8,128)} %param.12) | copy-start | bytes 3145732
  7.2 58.1 %reduce-scatter.2.cloned.1.call-start = ((), (), s32[]{:S(2)}) async-start(), calls=%async_computation.1 | async-start | bytes 4718592 | tf_op jit(solution)/shard_map/reduce_scatter | solution.py:33
Sparse Core Ops, SparseCore 0:
  11.4 53.8 reduce-scatter.1
